TPU v7x, 256 devices: a whole 4x4x8 slice. The times are simulated.
256 devices in a mesh: row: 32 (over z_hi, x, core), col: 8 (over y, z_lo).
Axes of the slice: x: 4, y: 4, z: 8 (z_hi: 4, z_lo: 2; z = z_hi * 2 + z_lo), core: 2. Of those that a mesh axis runs over, the one named last changes fastest.
Arguments:
- pivots: int32 [256], replicated, may hold values from 0 to 32767, as said below
- panel: float32 [32768, 256], P(('row', 'col')), may hold values from -6 to 6
- prior: bfloat16 [32768, 3072], P(('row', 'col')), may hold values from -0.796875 to 0.796875
- finished: bfloat16 [32768, 256], P(('row', 'col')), may hold values from -6 to 6
- pairs: int32 [32768], replicated, may hold values from 0 to 639999, as said below
- occupied: bfloat16 [800, 120], replicated, may hold values from -0.21875 to 0.21875
Outputs:
- updated: float32 [32768, 256], P(('row', 'col'))
- halves: float32 [256, 120, 800], P(('row', 'col'))
Inputs may be any that keep to these rules, and one draw needn't show every extreme that they name: `pivots`: distinct rows; at most 2 of them lie among the rows of one device (aligned blocks of 128 rows), and one device holds exactly 2. `pairs`: each value a * 800 + b with 0 <= b <= a < 800; all distinct and increasing.
All inputs are finite; a program needn't handle non-finite values.
Results may differ from a plain program's by a relative error of at most 0.0003.
Values may be sent and summed in bfloat16 or wider, within the bound.
A program may use at most 64 MiB of HBM per device.

v0:
```python
import jax
import jax.numpy as jnp
from jax import lax
from jax.sharding import PartitionSpec as P


def half_transform(received, pair_ids, occupied):
    orbitals = occupied.shape[0]
    pair_count = received.shape[0]
    vector_count = received.shape[1]
    first_ao = pair_ids // orbitals
    second_ao = pair_ids % orbitals
    off_diag = first_ao != second_ao
    occ_first = jnp.take(occupied, first_ao, axis=0)
    occ_second = jnp.where(
        off_diag[:, None], jnp.take(occupied, second_ao, axis=0), jnp.zeros((), jnp.bfloat16)
    )
    coeffs = jnp.concatenate([occ_first, occ_second], axis=0)
    targets = jnp.concatenate([second_ao, first_ao], axis=0).astype(jnp.int32)
    entries = jnp.concatenate([received, received], axis=0)
    doubled = 2 * pair_count
    wanted = min(doubled, max(1024, doubled // 8))
    block_rows = wanted
    for candidate in range(wanted, 0, -1):
        if doubled % candidate == 0:
            block_rows = candidate
            break
    columns = jnp.arange(orbitals, dtype=jnp.int32)

    def one_block(block_index, accumulated):
        start = block_index * block_rows
        coeff_block = lax.dynamic_slice_in_dim(coeffs, start, block_rows, 0)
        target_block = lax.dynamic_slice_in_dim(targets, start, block_rows, 0)
        entry_block = lax.dynamic_slice_in_dim(entries, start, block_rows, 0)
        matches = target_block[:, None] == columns[None, :]
        spread = jnp.where(
            matches[None, :, :], entry_block.T[:, :, None], jnp.zeros((), jnp.bfloat16)
        )
        return accumulated + jnp.einsum(
            "pi,vpm->vim", coeff_block, spread, preferred_element_type=jnp.float32
        )

    initial = jnp.zeros((vector_count, occupied.shape[1], orbitals), jnp.float32)
    return lax.fori_loop(0, doubled // block_rows, one_block, initial)


def per_device(pivots, panel, prior, finished, pairs, occupied):
    rows_dev = prior.shape[0]
    row_count = lax.axis_size("row")
    col_count = lax.axis_size("col")
    own_index = lax.axis_index("row") * col_count + lax.axis_index("col")
    owner = pivots // rows_dev
    local_rows = pivots % rows_dev
    owned = owner == own_index
    picked = jnp.take(prior, local_rows, axis=0).astype(jnp.float32)
    contribution = jnp.where(owned[:, None], picked, jnp.zeros_like(picked))
    pivot_rows = lax.psum(contribution, ("row", "col")).astype(jnp.bfloat16)
    updated = panel - lax.dot_general(
        prior, pivot_rows, (((1,), (1,)), ((), ())), preferred_element_type=jnp.float32
    )
    by_device = pairs.reshape(row_count, col_count, rows_dev)
    col_pairs = lax.dynamic_slice_in_dim(by_device, lax.axis_index("col"), 1, 1).reshape(-1)
    grouped = finished.reshape(rows_dev, row_count, finished.shape[1] // row_count)
    received = lax.all_to_all(grouped, "row", split_axis=1, concat_axis=0, tiled=True)
    partials = half_transform(
        received.reshape(received.shape[0], received.shape[2]), col_pairs, occupied
    )
    halves = lax.psum_scatter(partials, "col", scatter_dimension=0, tiled=True)
    return (updated, halves)


def solution(mesh):
    return jax.shard_map(
        per_device,
        mesh=mesh,
        in_specs=(
            P(),
            P(("row", "col"), None),
            P(("row", "col"), None),
            P(("row", "col"), None),
            P(),
            P(),
        ),
        out_specs=(P(("row", "col"), None), P(("row", "col"), None, None)),
        check_vma=False,
    )
```

profile of v0, /device:TPU:32, one launch (start us, length us, event | category | flops | bytes accessed | tf_op | source)
XLA Modules:
  0.0 254.6 jit_solution(17810283203826027613)
XLA Ops:
  7.2 0.0 copy-start
  7.2 0.0 copy-start.1
  7.2 1.7 copy.17
  8.9 10.4 %all-to-all-start = ((bf16[128,32,8]{0,2,1:T(8,128)(2,1)}), bf16[128,32,8]{0,2,1:T(8,128)(2,1)S(1)}, u32[]{:S(2)}, u32[]{:S(2)}) async-start(bf16[128,32,8]{0,2,1:T(8,128)(2,1)} %bitcast.4), calls=%async_computation | async-start | bytes 131072 | tf_op jit(solution)/shard_map/all_to_all | solution.py:64
  19.3 0.0 reduce-scatter.2.cloned.1.call-start
  19.3 1.0 broadcast_remainder_fusion
  20.3 1.0 compare_reduce_fusion
  21.4 0.0 copy-done.1
  21.4 12.1 %gather_fusion.2 = bf16[4096,120]{1,0:T(8,128)(2,1)S(1)} fusion(bf16[800,120]{1,0:T(8,128)(2,1)S(1)} %copy-done.1, s32[4096]{0:T(1024)S(1)} %get-tuple-element.172), kind=kCustom, calls=%fused_computation.1.clone | custom fusion | bytes 1982464 | tf_op jit(solution)/shard_map/jit(_take)/gather | solution.py:16
  33.5 12.1 %gather_fusion.1 = bf16[4096,120]{1,0:T(8,128)(2,1)S(1)} fusion(bf16[800,120]{1,0:T(8,128)(2,1)S(1)} %copy-done.1, s32[4096]{0:T(1024)S(1)} %fusion.21), kind=kCustom, calls=%fused_computation.clone | custom fusion | bytes 1982464 | tf_op jit(solution)/shard_map/jit(_take)/gather | solution.py:14
  45.7 2.1 broadcast_select_fusion
  47.8 1.4 select_select_fusion
  49.2 0.4 pad_maximum_fusion
  49.7 3.0 %copy.18 = bf16[8192,120]{0,1:T(8,128)(2,1)} copy(bf16[8192,120]{1,0:T(8,128)(2,1)S(1)} %pad_maximum_fusion) | data formatting | bytes 3932160
  52.6 0.0 all-to-all-done
  52.7 55.6 %while.14 = (s32[]{:T(128)}, f32[8,120,800]{1,2,0:T(8,128)}, s32[8192]{0:T(1024)S(1)}, bf16[8192,8]{0,1:T(8,128)(2,1)S(1)}, bf16[8192,120]{0,1:T(8,128)(2,1)}, /*index=5*/s32[]{:T(128)}, s32[]{:T(128)}, s32[]{:T(128)}, s32[]{:T(128)}) while((s32[]{:T(128)}, f32[8,120,800]{1,2,0:T(8,128)}, s32[8192]{0:T(1024)S(1)}, ...), condition=%wide.region_2.4_spmd.clone, body=%wide.region_1.3_spmd.clone.sunk | while | flops 1581772800 | bytes 8294561 | solution.py:44
  52.7 0.6 iota_compare_fusion.2
  53.3 5.9 %bitcast_add_fusion.2 = f32[8,120,800]{1,2,0:T(8,128)} fusion(f32[8,120,800]{1,2,0:T(8,128)} %get-tuple-element.216, pred[1024,800]{0,1:T(8,128)(4,1)S(1)} %iota_compare_fusion.2, bf16[8,1024]{1,0:T(8,128)(2,1)S(1)} %dynamic-slice_bitcast_fusion.2, pred[]{:T(512)S(6)} %compare.6, bf16[8192,120]{0,1:T(8,128)(2,1)} %get-tuple-element.228, ...), kind=kOutput, calls=%fused_computation.9.clone.1 | convolution fusion | flops 1580953600 | bytes 7430149 | tf_op jit(solution)/shard_map/while/body/eval_jaxpr/pi,vpm->vim/dot_general | solution.py:39
  59.2 0.6 iota_compare_fusion.2
  59.9 6.4 %bitcast_add_fusion.2 = f32[8,120,800]{1,2,0:T(8,128)} fusion(f32[8,120,800]{1,2,0:T(8,128)} %get-tuple-element.216, pred[1024,800]{0,1:T(8,128)(4,1)S(1)} %iota_compare_fusion.2, bf16[8,1024]{1,0:T(8,128)(2,1)S(1)} %dynamic-slice_bitcast_fusion.2, pred[]{:T(512)S(6)} %compare.6, bf16[8192,120]{0,1:T(8,128)(2,1)} %get-tuple-element.228, ...), kind=kOutput, calls=%fused_computation.9.clone.1 | convolution fusion | flops 1580953600 | bytes 7430149 | tf_op jit(solution)/shard_map/while/body/eval_jaxpr/pi,vpm->vim/dot_general | solution.py:39
  66.2 0.6 iota_compare_fusion.2
  66.9 6.4 %bitcast_add_fusion.2 = f32[8,120,800]{1,2,0:T(8,128)} fusion(f32[8,120,800]{1,2,0:T(8,128)} %get-tuple-element.216, pred[1024,800]{0,1:T(8,128)(4,1)S(1)} %iota_compare_fusion.2, bf16[8,1024]{1,0:T(8,128)(2,1)S(1)} %dynamic-slice_bitcast_fusion.2, pred[]{:T(512)S(6)} %compare.6, bf16[8192,120]{0,1:T(8,128)(2,1)} %get-tuple-element.228, ...), kind=kOutput, calls=%fused_computation.9.clone.1 | convolution fusion | flops 1580953600 | bytes 7430149 | tf_op jit(solution)/shard_map/while/body/eval_jaxpr/pi,vpm->vim/dot_general | solution.py:39
  73.2 0.6 iota_compare_fusion.2
  73.9 6.4 %bitcast_add_fusion.2 = f32[8,120,800]{1,2,0:T(8,128)} fusion(f32[8,120,800]{1,2,0:T(8,128)} %get-tuple-element.216, pred[1024,800]{0,1:T(8,128)(4,1)S(1)} %iota_compare_fusion.2, bf16[8,1024]{1,0:T(8,128)(2,1)S(1)} %dynamic-slice_bitcast_fusion.2, pred[]{:T(512)S(6)} %compare.6, bf16[8192,120]{0,1:T(8,128)(2,1)} %get-tuple-element.228, ...), kind=kOutput, calls=%fused_computation.9.clone.1 | convolution fusion | flops 1580953600 | bytes 7430149 | tf_op jit(solution)/shard_map/while/body/eval_jaxpr/pi,vpm->vim/dot_general | solution.py:39
  80.3 0.6 iota_compare_fusion.2
  80.9 6.4 %bitcast_add_fusion.2 = f32[8,120,800]{1,2,0:T(8,128)} fusion(f32[8,120,800]{1,2,0:T(8,128)} %get-tuple-element.216, pred[1024,800]{0,1:T(8,128)(4,1)S(1)} %iota_compare_fusion.2, bf16[8,1024]{1,0:T(8,128)(2,1)S(1)} %dynamic-slice_bitcast_fusion.2, pred[]{:T(512)S(6)} %compare.6, bf16[8192,120]{0,1:T(8,128)(2,1)} %get-tuple-element.228, ...), kind=kOutput, calls=%fused_computation.9.clone.1 | convolution fusion | flops 1580953600 | bytes 7430149 | tf_op jit(solution)/shard_map/while/body/eval_jaxpr/pi,vpm->vim/dot_general | solution.py:39
  87.3 0.6 iota_compare_fusion.2
  87.9 6.4 %bitcast_add_fusion.2 = f32[8,120,800]{1,2,0:T(8,128)} fusion(f32[8,120,800]{1,2,0:T(8,128)} %get-tuple-element.216, pred[1024,800]{0,1:T(8,128)(4,1)S(1)} %iota_compare_fusion.2, bf16[8,1024]{1,0:T(8,128)(2,1)S(1)} %dynamic-slice_bitcast_fusion.2, pred[]{:T(512)S(6)} %compare.6, bf16[8192,120]{0,1:T(8,128)(2,1)} %get-tuple-element.228, ...), kind=kOutput, calls=%fused_computation.9.clone.1 | convolution fusion | flops 1580953600 | bytes 7430149 | tf_op jit(solution)/shard_map/while/body/eval_jaxpr/pi,vpm->vim/dot_general | solution.py:39
  94.3 0.6 iota_compare_fusion.2
  94.9 6.4 %bitcast_add_fusion.2 = f32[8,120,800]{1,2,0:T(8,128)} fusion(f32[8,120,800]{1,2,0:T(8,128)} %get-tuple-element.216, pred[1024,800]{0,1:T(8,128)(4,1)S(1)} %iota_compare_fusion.2, bf16[8,1024]{1,0:T(8,128)(2,1)S(1)} %dynamic-slice_bitcast_fusion.2, pred[]{:T(512)S(6)} %compare.6, bf16[8192,120]{0,1:T(8,128)(2,1)} %get-tuple-element.228, ...), kind=kOutput, calls=%fused_computation.9.clone.1 | convolution fusion | flops 1580953600 | bytes 7430149 | tf_op jit(solution)/shard_map/while/body/eval_jaxpr/pi,vpm->vim/dot_general | solution.py:39
  101.3 0.6 iota_compare_fusion.2
  101.9 6.4 %bitcast_add_fusion.2 = f32[8,120,800]{1,2,0:T(8,128)} fusion(f32[8,120,800]{1,2,0:T(8,128)} %get-tuple-element.216, pred[1024,800]{0,1:T(8,128)(4,1)S(1)} %iota_compare_fusion.2, bf16[8,1024]{1,0:T(8,128)(2,1)S(1)} %dynamic-slice_bitcast_fusion.2, pred[]{:T(512)S(6)} %compare.6, bf16[8192,120]{0,1:T(8,128)(2,1)} %get-tuple-element.228, ...), kind=kOutput, calls=%fused_computation.9.clone.1 | convolution fusion | flops 1580953600 | bytes 7430149 | tf_op jit(solution)/shard_map/while/body/eval_jaxpr/pi,vpm->vim/dot_general | solution.py:39
  108.3 0.0 copy-start.3
  108.3 0.0 reduce-scatter.2.cloned.1.call-update
  108.3 0.6 copy-done.3
  109.0 0.0 copy-done
  109.0 1.6 gather_fusion
  110.6 0.0 copy-start.2
  110.6 2.4 convert_select_fusion
  113.0 0.0 copy-done.2
  113.0 0.1 copy.16
  113.1 133.3 %all-reduce.1 = bf16[256,3072]{1,0:T(8,128)(2,1)S(1)} all-reduce(f32[256,3072]{1,0:T(8,128)} %convert_select_fusion), channel_id=1, replica_groups=mesh['row'=32,'col'=8] {'row','col'}, use_global_device_ids=true, to_apply=%region_0.1 | all-reduce | flops 786432 | bytes 4718592 | tf_op jit(solution)/shard_map/psum | solution.py:57
  246.4 0.6 fusion.18
  247.0 0.8 copy.19
  247.7 0.0 reduce-scatter.2.cloned.1.call-done
  (25 shorter events, 0.2 us)
Async XLA Ops:
  7.2 101.8 %copy-start = (bf16[128,3072]{1,0:T(8,128)(2,1)S(1)}, bf16[128,3072]{1,0:T(8,128)(2,1)}, u32[]{:S(2)}) copy-start(bf16[128,3072]{1,0:T(8,128)(2,1)} %param.12) | copy-start | bytes 2359300
  7.2 14.2 %copy-start.1 = (bf16[800,120]{1,0:T(8,128)(2,1)S(1)}, bf16[800,120]{1,0:T(8,128)(2,1)}, u32[]{:S(2)}) copy-start(bf16[800,120]{1,0:T(8,128)(2,1)} %param.15) | copy-start | bytes 576004
  8.9 43.8 %all-to-all-start = ((bf16[128,32,8]{0,2,1:T(8,128)(2,1)}), bf16[128,32,8]{0,2,1:T(8,128)(2,1)S(1)}, u32[]{:S(2)}, u32[]{:S(2)}) async-start(bf16[128,32,8]{0,2,1:T(8,128)(2,1)} %bitcast.4), calls=%async_computation | async-start | bytes 131072 | tf_op jit(solution)/shard_map/all_to_all | solution.py:64
  19.3 228.5 %reduce-scatter.2.cloned.1.call-start = ((), (), s32[]{:S(2)}) async-start(), calls=%async_computation.2 | async-start | bytes 3686400 | tf_op jit(solution)/shard_map/reduce_scatter | solution.py:68
  108.3 0.7 copy-start.3
  110.6 2.4 copy-start.2
Sparse Core Ops, SparseCore 0:
  108.4 78.8 reduce-scatter.1
where the time goes:
time: 255 us
  blocking collectives  133 us (52%)
  matrix products  51.2 us (20%)
  local copies, waits for them, and re-layouts  32.1 us (13%)
  between operations  14.2 us (6%)
  other arithmetic  13.1 us (5%)
  starting transfers between devices  10.5 us (4%)
    psum x1, blocking collectives, per_device(): pivot_rows = lax.psum(contribution, ('row', 'col')).astype(jnp.bfloat16)  133 us
    dot_general x8, matrix products, one_block(): jnp.einsum('pi,vpm->vim', coeff_block, spread, preferred_element_type=jnp...  50.6 us
    gather x1, local copies, waits for them, and re-layouts, half_transform(): jnp.take(occupied, second_ao, axis=0)  12.1 us
    gather x1, local copies, waits for them, and re-layouts, half_transform(): occ_first = jnp.take(occupied, first_ao, axis=0)  12.1 us
    all_to_all x1, starting transfers between devices, per_device(): lax.all_to_all(grouped, 'row', split_axis=1, concat_axis=0, tiled=True)  10.4 us
    unnamed x12, local copies, waits for them, and re-layouts  6.15 us
  transfers between devices with their start and end apart: 2, of which 0 were waited for; matrix products, arithmetic and copies ran while one was open for 15% of the time, Pallas kernels for 0%

commit v1 on v0

--- a/solution.py
+++ b/solution.py
@@ -54,7 +54,7 @@
     owned = owner == own_index
     picked = jnp.take(prior, local_rows, axis=0).astype(jnp.float32)
     contribution = jnp.where(owned[:, None], picked, jnp.zeros_like(picked))
-    pivot_rows = lax.psum(contribution, ("row", "col")).astype(jnp.bfloat16)
+    pivot_rows = lax.psum(lax.psum(contribution, "row"), "col").astype(jnp.bfloat16)
     updated = panel - lax.dot_general(
         prior, pivot_rows, (((1,), (1,)), ((), ())), preferred_element_type=jnp.float32
     )

time: 255 us -> 497 us (1.95)
  waiting for transfers between devices: 0.02 us -> 249 us
  blocking collectives: 133 us -> 124 us
    psum x0 -> x1, waiting for transfers between devices: none -> 248 us  [per_device(): lax.psum(contribution, 'row')]
    psum x1, blocking collectives: 133 us -> 124 us  [per_device(): lax.psum(lax.psum(contribution, 'row'), 'col').astype(jnp.bfloat16)]
  transfers between devices with their start and end apart: 2 -> 3, of which waited for: 0 -> 1; matrix products, arithmetic and copies ran while one was open for 15% -> 19% of each run, Pallas kernels for 0% -> 0%
where the time goes in v1:
time: 497 us
  waiting for transfers between devices  249 us (50%)
  blocking collectives  124 us (25%)
  matrix products  51.5 us (10%)
  local copies, waits for them, and re-layouts  32.2 us (6%)
  between operations  15.7 us (3%)
  other arithmetic  13.9 us (3%)
  starting transfers between devices  10.5 us (2%)
    psum x1, waiting for transfers between devices, per_device(): lax.psum(contribution, 'row')  248 us
    psum x1, blocking collectives, per_device(): lax.psum(lax.psum(contribution, 'row'), 'col').astype(jnp.bfloat16)  124 us
    dot_general x8, matrix products, one_block(): jnp.einsum('pi,vpm->vim', coeff_block, spread, preferred_element_type=jnp...  50.9 us
    gather x1, local copies, waits for them, and re-layouts, half_transform(): jnp.take(occupied, second_ao, axis=0)  12.1 us
    gather x1, local copies, waits for them, and re-layouts, half_transform(): occ_first = jnp.take(occupied, first_ao, axis=0)  12.1 us
    all_to_all x1, starting transfers between devices, per_device(): lax.all_to_all(grouped, 'row', split_axis=1, concat_axis=0, tiled=True)  10.4 us
  transfers between devices with their start and end apart: 3, of which 1 were waited for; matrix products, arithmetic and copies ran while one was open for 19% of the time, Pallas kernels for 0%

profile of v1, /device:TPU:32, one launch (start us, length us, event | category | flops | bytes accessed | tf_op | source)
XLA Modules:
  0.0 496.7 jit_solution(16590286378519993348)
XLA Ops:
  8.0 0.0 copy-start
  8.0 1.6 copy.17
  9.7 10.4 %all-to-all-start = ((bf16[128,32,8]{0,2,1:T(8,128)(2,1)}), bf16[128,32,8]{0,2,1:T(8,128)(2,1)S(1)}, u32[]{:S(2)}, u32[]{:S(2)}) async-start(bf16[128,32,8]{0,2,1:T(8,128)(2,1)} %bitcast.4), calls=%async_computation | async-start | bytes 131072 | tf_op jit(solution)/shard_map/all_to_all | solution.py:64
  20.1 0.0 all-reduce.3.cloned.1.call-start
  20.1 0.7 compare_and_fusion.2
  20.8 0.0 copy-done
  20.9 1.6 gather_fusion
  22.4 0.0 copy-start.1
  22.4 2.4 convert_select_fusion
  24.9 0.0 all-reduce.3.cloned.1.call-update
  24.9 0.0 reduce-scatter.2.cloned.1.call-start
  24.9 1.0 broadcast_remainder_fusion
  25.9 1.0 compare_reduce_fusion
  27.0 0.0 copy-done.1
  27.0 12.1 %gather_fusion.2 = bf16[4096,120]{1,0:T(8,128)(2,1)S(1)} fusion(bf16[800,120]{1,0:T(8,128)(2,1)S(1)} %copy-done.1, s32[4096]{0:T(1024)S(1)} %get-tuple-element.172), kind=kCustom, calls=%fused_computation.1.clone | custom fusion | bytes 1982464 | tf_op jit(solution)/shard_map/jit(_take)/gather | solution.py:16
  39.1 12.1 %gather_fusion.1 = bf16[4096,120]{1,0:T(8,128)(2,1)S(1)} fusion(bf16[800,120]{1,0:T(8,128)(2,1)S(1)} %copy-done.1, s32[4096]{0:T(1024)S(1)} %fusion.21), kind=kCustom, calls=%fused_computation.clone | custom fusion | bytes 1982464 | tf_op jit(solution)/shard_map/jit(_take)/gather | solution.py:14
  51.3 2.1 broadcast_select_fusion
  53.4 1.4 select_select_fusion
  54.9 0.4 pad_maximum_fusion
  55.3 2.9 copy.18
  58.2 0.0 all-to-all-done
  58.2 55.9 %while.14 = (s32[]{:T(128)}, f32[8,120,800]{1,2,0:T(8,128)}, s32[8192]{0:T(1024)S(1)}, bf16[8192,8]{0,1:T(8,128)(2,1)S(1)}, bf16[8192,120]{0,1:T(8,128)(2,1)}, /*index=5*/s32[]{:T(128)}, s32[]{:T(128)}, s32[]{:T(128)}, s32[]{:T(128)}) while((s32[]{:T(128)}, f32[8,120,800]{1,2,0:T(8,128)}, s32[8192]{0:T(1024)S(1)}, ...), condition=%wide.region_3.5_spmd.clone, body=%wide.region_2.4_spmd.clone.sunk | while | flops 1581772800 | bytes 8294561 | solution.py:44
  58.2 0.6 iota_compare_fusion.2
  58.9 5.9 %bitcast_add_fusion.2 = f32[8,120,800]{1,2,0:T(8,128)} fusion(f32[8,120,800]{1,2,0:T(8,128)} %get-tuple-element.216, pred[1024,800]{0,1:T(8,128)(4,1)S(1)} %iota_compare_fusion.2, bf16[8,1024]{1,0:T(8,128)(2,1)S(1)} %dynamic-slice_bitcast_fusion.2, pred[]{:T(512)S(6)} %compare.6, bf16[8192,120]{0,1:T(8,128)(2,1)} %get-tuple-element.228, ...), kind=kOutput, calls=%fused_computation.9.clone.1 | convolution fusion | flops 1580953600 | bytes 7430149 | tf_op jit(solution)/shard_map/while/body/eval_jaxpr/pi,vpm->vim/dot_general | solution.py:39
  64.8 0.6 iota_compare_fusion.2
  65.4 6.4 %bitcast_add_fusion.2 = f32[8,120,800]{1,2,0:T(8,128)} fusion(f32[8,120,800]{1,2,0:T(8,128)} %get-tuple-element.216, pred[1024,800]{0,1:T(8,128)(4,1)S(1)} %iota_compare_fusion.2, bf16[8,1024]{1,0:T(8,128)(2,1)S(1)} %dynamic-slice_bitcast_fusion.2, pred[]{:T(512)S(6)} %compare.6, bf16[8192,120]{0,1:T(8,128)(2,1)} %get-tuple-element.228, ...), kind=kOutput, calls=%fused_computation.9.clone.1 | convolution fusion | flops 1580953600 | bytes 7430149 | tf_op jit(solution)/shard_map/while/body/eval_jaxpr/pi,vpm->vim/dot_general | solution.py:39
  71.9 0.6 iota_compare_fusion.2
  72.5 6.4 %bitcast_add_fusion.2 = f32[8,120,800]{1,2,0:T(8,128)} fusion(f32[8,120,800]{1,2,0:T(8,128)} %get-tuple-element.216, pred[1024,800]{0,1:T(8,128)(4,1)S(1)} %iota_compare_fusion.2, bf16[8,1024]{1,0:T(8,128)(2,1)S(1)} %dynamic-slice_bitcast_fusion.2, pred[]{:T(512)S(6)} %compare.6, bf16[8192,120]{0,1:T(8,128)(2,1)} %get-tuple-element.228, ...), kind=kOutput, calls=%fused_computation.9.clone.1 | convolution fusion | flops 1580953600 | bytes 7430149 | tf_op jit(solution)/shard_map/while/body/eval_jaxpr/pi,vpm->vim/dot_general | solution.py:39
  78.9 0.6 iota_compare_fusion.2
  79.5 6.4 %bitcast_add_fusion.2 = f32[8,120,800]{1,2,0:T(8,128)} fusion(f32[8,120,800]{1,2,0:T(8,128)} %get-tuple-element.216, pred[1024,800]{0,1:T(8,128)(4,1)S(1)} %iota_compare_fusion.2, bf16[8,1024]{1,0:T(8,128)(2,1)S(1)} %dynamic-slice_bitcast_fusion.2, pred[]{:T(512)S(6)} %compare.6, bf16[8192,120]{0,1:T(8,128)(2,1)} %get-tuple-element.228, ...), kind=kOutput, calls=%fused_computation.9.clone.1 | convolution fusion | flops 1580953600 | bytes 7430149 | tf_op jit(solution)/shard_map/while/body/eval_jaxpr/pi,vpm->vim/dot_general | solution.py:39
  86.0 0.6 iota_compare_fusion.2
  86.6 6.4 %bitcast_add_fusion.2 = f32[8,120,800]{1,2,0:T(8,128)} fusion(f32[8,120,800]{1,2,0:T(8,128)} %get-tuple-element.216, pred[1024,800]{0,1:T(8,128)(4,1)S(1)} %iota_compare_fusion.2, bf16[8,1024]{1,0:T(8,128)(2,1)S(1)} %dynamic-slice_bitcast_fusion.2, pred[]{:T(512)S(6)} %compare.6, bf16[8192,120]{0,1:T(8,128)(2,1)} %get-tuple-element.228, ...), kind=kOutput, calls=%fused_computation.9.clone.1 | convolution fusion | flops 1580953600 | bytes 7430149 | tf_op jit(solution)/shard_map/while/body/eval_jaxpr/pi,vpm->vim/dot_general | solution.py:39
  93.0 0.6 iota_compare_fusion.2
  93.6 6.4 %bitcast_add_fusion.2 = f32[8,120,800]{1,2,0:T(8,128)} fusion(f32[8,120,800]{1,2,0:T(8,128)} %get-tuple-element.216, pred[1024,800]{0,1:T(8,128)(4,1)S(1)} %iota_compare_fusion.2, bf16[8,1024]{1,0:T(8,128)(2,1)S(1)} %dynamic-slice_bitcast_fusion.2, pred[]{:T(512)S(6)} %compare.6, bf16[8192,120]{0,1:T(8,128)(2,1)} %get-tuple-element.228, ...), kind=kOutput, calls=%fused_computation.9.clone.1 | convolution fusion | flops 1580953600 | bytes 7430149 | tf_op jit(solution)/shard_map/while/body/eval_jaxpr/pi,vpm->vim/dot_general | solution.py:39
  100.0 0.6 iota_compare_fusion.2
  100.7 6.4 %bitcast_add_fusion.2 = f32[8,120,800]{1,2,0:T(8,128)} fusion(f32[8,120,800]{1,2,0:T(8,128)} %get-tuple-element.216, pred[1024,800]{0,1:T(8,128)(4,1)S(1)} %iota_compare_fusion.2, bf16[8,1024]{1,0:T(8,128)(2,1)S(1)} %dynamic-slice_bitcast_fusion.2, pred[]{:T(512)S(6)} %compare.6, bf16[8192,120]{0,1:T(8,128)(2,1)} %get-tuple-element.228, ...), kind=kOutput, calls=%fused_computation.9.clone.1 | convolution fusion | flops 1580953600 | bytes 7430149 | tf_op jit(solution)/shard_map/while/body/eval_jaxpr/pi,vpm->vim/dot_general | solution.py:39
  107.1 0.6 iota_compare_fusion.2
  107.7 6.4 %bitcast_add_fusion.2 = f32[8,120,800]{1,2,0:T(8,128)} fusion(f32[8,120,800]{1,2,0:T(8,128)} %get-tuple-element.216, pred[1024,800]{0,1:T(8,128)(4,1)S(1)} %iota_compare_fusion.2, bf16[8,1024]{1,0:T(8,128)(2,1)S(1)} %dynamic-slice_bitcast_fusion.2, pred[]{:T(512)S(6)} %compare.6, bf16[8192,120]{0,1:T(8,128)(2,1)} %get-tuple-element.228, ...), kind=kOutput, calls=%fused_computation.9.clone.1 | convolution fusion | flops 1580953600 | bytes 7430149 | tf_op jit(solution)/shard_map/while/body/eval_jaxpr/pi,vpm->vim/dot_general | solution.py:39
  114.1 0.0 copy-start.2
  114.1 0.0 reduce-scatter.2.cloned.1.call-update
  114.2 0.9 copy-done.2
  115.0 0.1 copy.16
  115.1 248.5 %all-reduce.3.cloned.1.call-done = f32[256,3072]{1,0:T(8,128)} async-done(((f32[256,3072]{1,0:T(8,128)}), f32[256,3072]{1,0:T(8,128)}) %all-reduce.3.cloned.1.call-update) | async-done | bytes 3145744 | tf_op jit(solution)/shard_map/psum | solution.py:57
  363.6 124.2 %all-reduce.4 = bf16[256,3072]{1,0:T(8,128)(2,1)S(1)} all-reduce(f32[256,3072]{1,0:T(8,128)} %all-reduce.3.cloned.1.call-done), channel_id=1, replica_groups=mesh['row'=32,'col'=8] {'col'}, use_global_device_ids=true, to_apply=%region_1.2 | all-reduce | flops 786432 | bytes 4718592 | tf_op jit(solution)/shard_map/psum | solution.py:57
  487.9 0.6 fusion.18
  488.4 0.8 copy.19
  489.2 0.0 reduce-scatter.2.cloned.1.call-done
  (24 shorter events, 0.2 us)
Async XLA Ops:
  8.0 12.9 %copy-start = (bf16[128,3072]{1,0:T(8,128)(2,1)S(1)}, bf16[128,3072]{1,0:T(8,128)(2,1)}, u32[]{:S(2)}) copy-start(bf16[128,3072]{1,0:T(8,128)(2,1)} %param.12) | copy-start | bytes 2359300
  9.7 48.5 %all-to-all-start = ((bf16[128,32,8]{0,2,1:T(8,128)(2,1)}), bf16[128,32,8]{0,2,1:T(8,128)(2,1)S(1)}, u32[]{:S(2)}, u32[]{:S(2)}) async-start(bf16[128,32,8]{0,2,1:T(8,128)(2,1)} %bitcast.4), calls=%async_computation | async-start | bytes 131072 | tf_op jit(solution)/shard_map/all_to_all | solution.py:64
  20.1 343.6 %all-reduce.3.cloned.1.call-start = ((), (), s32[]{:S(2)}) async-start(), calls=%async_computation.2 | async-start | bytes 6291456 | tf_op jit(solution)/shard_map/psum | solution.py:57
  22.4 4.6 copy-start.1
  24.9 464.3 %reduce-scatter.2.cloned.1.call-start = ((), (), s32[]{:S(2)}) async-start(), calls=%async_computation.3 | async-start | bytes 3686400 | tf_op jit(solution)/shard_map/reduce_scatter | solution.py:68
  114.1 0.9 copy-start.2
Sparse Core Ops, SparseCore 0:
  25.0 338.5 all-reduce.2
Sparse Core Ops, SparseCore 1:
  114.3 83.2 reduce-scatter.1
